TPU v7x, 32 devices: a whole 2x2x4 slice. The times are simulated.
32 devices in a mesh: tp: 8 (over z, y), kv: 4 (over x, core).
Axes of the slice: x: 2, y: 2, z: 4, core: 2. Of those that a mesh axis runs over, the one named last changes fastest.
Arguments:
- hidden_in: bfloat16 [2048, 4096], P(('kv', 'tp')), may hold values from -6 to 6
- gain_attn: float32 [4096], replicated, may hold values from 0.4 to 1.6
- w_qkv: bfloat16 [4096, 32, 384], P(None, 'tp'), may hold values from -0.09375 to 0.09375
- cache_kv: bfloat16 [2, 8192, 32, 256], P(None, 'kv', 'tp'), may hold values from -110 to 110
- cache_len: int32 [2], replicated, may hold values from 128 to 8192, as said below
- w_out: bfloat16 [4096, 4096], P('tp'), may hold values from -0.1875 to 0.1875
- gain_mlp: float32 [4096], replicated, may hold values from 0.1 to 1.9
- w_gate_up: bfloat16 [4096, 2, 11008], P('kv', None, 'tp'), may hold values from -0.09375 to 0.09375
- w_down: bfloat16 [11008, 4096], P('tp', 'kv'), may hold values from -0.0546875 to 0.0546875
Outputs:
- layer_out: bfloat16 [2048, 4096], P(('kv', 'tp'))
Inputs may be any that keep to these rules, and one draw needn't show every extreme that they name: `cache_len`: every length is a multiple of 128; some sequence uses the whole cache.
All inputs are finite; a program needn't handle non-finite values.
Results may differ from a plain program's by a relative error of at most 0.019.
The roundings to bfloat16 on the way count: a program that leaves them out, or rounds other values in their place, can miss the bound.
Values may be sent and summed in bfloat16 or wider, within the bound.
A program may use at most 192 MiB of HBM per device.

v0:
```python
import math
import jax
import jax.numpy as jnp
from jax import lax
from jax.sharding import PartitionSpec as P

EPSILON = 1e-05
MASKED = -1e30


def rms_scale(values_in, gain_vector):
    widened = values_in.astype(jnp.float32)
    mean_square = jnp.mean(widened * widened, axis=-1, keepdims=True)
    return (widened * lax.rsqrt(mean_square + EPSILON) * gain_vector).astype(jnp.bfloat16)


def per_device(
    hidden_in, gain_attn, w_qkv, cache_kv, cache_len, w_out, gain_mlp, w_gate_up, w_down
):
    local_heads = w_qkv.shape[1]
    head_dim = w_qkv.shape[2] // 3
    own_rows = hidden_in.shape[0]
    block_input = lax.all_gather(hidden_in, "tp", axis=0, tiled=True)
    block_rows = block_input.shape[0]
    normed = rms_scale(block_input, gain_attn)
    flat_qkv = w_qkv.reshape(w_qkv.shape[0], local_heads * 3 * head_dim)
    packed = jnp.dot(normed, flat_qkv, preferred_element_type=jnp.float32).astype(jnp.bfloat16)
    packed = packed.reshape(block_rows, local_heads, 3 * head_dim)
    key_mine = packed[:, :, head_dim : 2 * head_dim]
    value_mine = packed[:, :, 2 * head_dim :]
    query_rows = lax.all_gather(packed[:, :, :head_dim], "kv", axis=0, tiled=True)
    seq_count = cache_kv.shape[0]
    span_len = query_rows.shape[0] // seq_count
    kv_index = lax.axis_index("kv")
    cache_rows = cache_kv.shape[1]
    cache_pos = kv_index * cache_rows + jnp.arange(cache_rows, dtype=jnp.int32)
    own_seq = (kv_index * block_rows + jnp.arange(block_rows, dtype=jnp.int32)) // span_len
    row_peaks, masses, accums = ([], [], [])
    for seq_id in range(seq_count):
        query_block = query_rows[seq_id * span_len : (seq_id + 1) * span_len]
        joined_key_rows = jnp.concatenate([cache_kv[seq_id, :, :, :head_dim], key_mine], axis=0)
        joined_value_rows = jnp.concatenate([cache_kv[seq_id, :, :, head_dim:], value_mine], axis=0)
        usable = jnp.concatenate([cache_pos < cache_len[seq_id], own_seq == seq_id])
        logit_scores = jnp.einsum(
            "qhd,khd->hqk", query_block, joined_key_rows, preferred_element_type=jnp.float32
        ) / math.sqrt(head_dim)
        logit_scores = jnp.where(usable[None, None, :], logit_scores, MASKED)
        row_peak = jnp.max(logit_scores, axis=2)
        raw_weights = jnp.where(
            usable[None, None, :], jnp.exp(logit_scores - row_peak[:, :, None]), 0.0
        )
        row_peaks.append(row_peak.T)
        masses.append(jnp.sum(raw_weights, axis=2).T)
        accums.append(
            jnp.einsum(
                "hqk,khd->qhd",
                raw_weights.astype(jnp.bfloat16),
                joined_value_rows,
                preferred_element_type=jnp.float32,
            )
        )
    peak_all = jnp.concatenate(row_peaks, axis=0)
    mass_all = jnp.concatenate(masses, axis=0)
    accum_all = jnp.concatenate(accums, axis=0)
    peak_set, mass_set, accum_set = (
        lax.all_to_all(peak_all[None], "kv", split_axis=1, concat_axis=0, tiled=True),
        lax.all_to_all(mass_all[None], "kv", split_axis=1, concat_axis=0, tiled=True),
        lax.all_to_all(accum_all[None], "kv", split_axis=1, concat_axis=0, tiled=True),
    )
    peak_best = jnp.max(peak_set, axis=0)
    scaling = jnp.exp(peak_set - peak_best[None])
    mass_own = jnp.sum(mass_set * scaling, axis=0)
    accum_own = jnp.sum(accum_set * scaling[..., None], axis=0)
    attended = (
        (accum_own / mass_own[..., None])
        .astype(jnp.bfloat16)
        .reshape(block_rows, local_heads * head_dim)
    )
    tp_index = lax.axis_index("tp")
    heads_sum = lax.psum(
        jnp.dot(attended, w_out, preferred_element_type=jnp.float32).astype(jnp.bfloat16), "tp"
    ).astype(jnp.float32)
    residual = block_input.astype(jnp.float32) + heads_sum
    mlp_in = rms_scale(residual, gain_mlp)
    residual_own = lax.dynamic_slice_in_dim(residual, tp_index * own_rows, own_rows, 0)
    gate_up = jnp.einsum(
        "td,dgf->tgf",
        mlp_in,
        lax.all_gather(w_gate_up, "kv", axis=0, tiled=True),
        preferred_element_type=jnp.float32,
    )
    activated = (jax.nn.silu(gate_up[:, 0, :]) * gate_up[:, 1, :]).astype(jnp.bfloat16)
    down_terms = jnp.dot(
        activated,
        lax.all_gather(w_down, "kv", axis=1, tiled=True),
        preferred_element_type=jnp.float32,
    )
    down_own = lax.psum_scatter(
        down_terms.astype(jnp.bfloat16), "tp", scatter_dimension=0, tiled=True
    ).astype(jnp.float32)
    return (residual_own + down_own).astype(jnp.bfloat16)


def solution(mesh):
    in_specs = (
        P(("kv", "tp"), None),
        P(),
        P(None, "tp", None),
        P(None, "kv", "tp", None),
        P(),
        P("tp", None),
        P(),
        P("kv", None, "tp"),
        P("tp", "kv"),
    )
    out_specs = P(("kv", "tp"), None)
    return jax.shard_map(
        per_device, mesh=mesh, in_specs=in_specs, out_specs=out_specs, check_vma=False
    )
```

profile of v0, /device:TPU:0, one launch (start us, length us, event | category | flops | bytes accessed | tf_op | source)
XLA Modules:
  0.0 827.3 jit_solution(16002876231132787441)
XLA Ops:
  6.5 0.7 all-gather.5.cloned.1.call-update
  7.3 12.4 %copy.51 = bf16[512,8,4,384]{3,1,2,0:T(8,128)(2,1)} copy(bf16[512,8,4,384]{3,2,1,0:T(4,128)(2,1)} %bitcast.50) | data formatting | bytes 25165824
  19.7 65.3 %all-gather.5.cloned.1.call-done = bf16[512,4096]{1,0:T(8,128)(2,1)} async-done(((bf16[64,4096]{1,0:T(8,128)(2,1)}), bf16[512,4096]{1,0:T(8,128)(2,1)}) %all-gather.5.cloned.1.call-update) | async-done | bytes 4194320 | tf_op jit(solution)/shard_map/all_gather | solution.py:23
  85.0 3.1 fusion.12
  88.1 11.0 %fusion.24 = bf16[512,1536]{1,0:T(8,128)(2,1)S(1)} fusion(bf16[4096,1536]{1,0:T(8,128)(2,1)} %bitcast.51, bf16[512,4096]{1,0:T(8,128)(2,1)} %all-gather.5.cloned.1.call-done, f32[4096]{0:T(1024)S(1)} %copy-done.5, f32[512]{0:T(512)S(1)} %add_rsqrt_fusion.1), kind=kOutput, calls=%fused_computation.37 | convolution fusion | flops 6451625984 | bytes 18368512 | tf_op jit(solution)/shard_map/dot_general | solution.py:27
  99.5 0.5 fusion.62
  100.0 0.9 copy.46
  100.9 6.4 fusion.61
  107.4 4.4 copy.44
  111.8 2.6 copy.49
  114.4 0.6 fusion.63
  115.0 1.3 fusion.45
  116.3 4.1 copy_bitcast_fusion
  120.4 1.1 copy.45
  121.6 0.6 all-gather.7.cloned.1.call-done
  122.2 19.7 %fusion.1 = (f32[4,1024]{1,0:T(4,128)S(1)}, f32[4,1024,2560]{2,1,0:T(8,128)}) fusion(pred[2560]{0:T(1024)(128)(4,1)S(1)} %pad_add_fusion.1, bf16[512,4,128]{2,0,1:T(8,128)(2,1)S(1)} %copy.48, bf16[2048,4,128]{2,0,1:T(8,128)(2,1)} %get-tuple-element.26, bf16[2048,4,128]{2,0,1:T(8,128)(2,1)} %all-gather.7.cloned.1.call-done), kind=kOutput, calls=%fused_computation.5 | convolution fusion | flops 2721050624 | bytes 45632000 | tf_op jit(solution)/shard_map/qhd,khd->hqk/dot_general | solution.py:44
  141.8 19.2 %fusion.4 = f32[4,1024]{1,0:T(4,128)S(1)} fusion(f32[4,1024,2560]{2,1,0:T(8,128)} %get-tuple-element.19, f32[4,1024]{1,0:T(4,128)S(1)} %get-tuple-element.18, pred[2560]{0:T(1024)(128)(4,1)S(1)} %pad_add_fusion.1), kind=kLoop, calls=%fused_computation.8 | loop fusion | flops 52424704 | bytes 41978368 | tf_op jit(solution)/shard_map/reduce_sum | solution.py:53
  161.1 17.9 %fusion.38 = f32[1024,4,128]{0,2,1:T(8,128)} fusion(f32[4,1024,2560]{2,1,0:T(8,128)} %get-tuple-element.19, f32[4,1024]{1,0:T(4,128)S(1)} %get-tuple-element.18, pred[2560]{0:T(1024)(128)(4,1)S(1)} %pad_add_fusion.1, bf16[512,4,128]{0,2,1:T(8,128)(2,1)S(1)} %copy-done.3, bf16[2048,4,128]{0,2,1:T(8,128)(2,1)S(1)} %bitcast.59), kind=kOutput, calls=%fused_computation.51 | convolution fusion | flops 2742026240 | bytes 46680576 | tf_op jit(solution)/shard_map/hqk,khd->qhd/dot_general | solution.py:55
  178.9 19.0 %fusion = (f32[4,1024]{1,0:T(4,128)S(1)}, f32[4,1024,2560]{2,1,0:T(8,128)}) fusion(pred[2560]{0:T(1024)(128)(4,1)S(1)} %pad_add_fusion, bf16[512,4,128]{2,0,1:T(8,128)(2,1)S(1)} %copy.48, bf16[2048,4,128]{2,0,1:T(8,128)(2,1)S(1)} %get-tuple-element.27, bf16[2048,4,128]{2,0,1:T(8,128)(2,1)} %all-gather.7.cloned.1.call-done), kind=kOutput, calls=%fused_computation.4 | convolution fusion | flops 2721050624 | bytes 45632000 | tf_op jit(solution)/shard_map/qhd,khd->hqk/dot_general | solution.py:44
  198.0 19.2 %fusion.2 = f32[4,1024]{1,0:T(4,128)S(1)} fusion(f32[4,1024,2560]{2,1,0:T(8,128)} %get-tuple-element.21, f32[4,1024]{1,0:T(4,128)S(1)} %get-tuple-element.20, pred[2560]{0:T(1024)(128)(4,1)S(1)} %pad_add_fusion), kind=kLoop, calls=%fused_computation.6 | loop fusion | flops 52424704 | bytes 41978368 | tf_op jit(solution)/shard_map/reduce_sum | solution.py:53
  217.2 17.9 %fusion.35 = f32[1024,4,128]{0,2,1:T(8,128)} fusion(f32[4,1024,2560]{2,1,0:T(8,128)} %get-tuple-element.21, f32[4,1024]{1,0:T(4,128)S(1)} %get-tuple-element.20, pred[2560]{0:T(1024)(128)(4,1)S(1)} %pad_add_fusion, bf16[512,4,128]{0,2,1:T(8,128)(2,1)S(1)} %copy-done.3, bf16[2048,4,128]{0,2,1:T(8,128)(2,1)S(1)} %bitcast.58), kind=kOutput, calls=%fused_computation.50 | convolution fusion | flops 2742026240 | bytes 46680576 | tf_op jit(solution)/shard_map/hqk,khd->qhd/dot_general | solution.py:55
  235.5 0.6 broadcast.98
  236.1 9.5 %reduce.2 = f32[2048,4]{1,0:T(8,128)S(1)} reduce(f32[2048,1,4]{2,1,0:T(1,128)S(1)} %bitcast.54, f32[]{:T(128)} %broadcast.98), dimensions={1}, to_apply=%bitcast.41.reduce_sub_computation | reduce | bytes 65540
  245.6 1.3 reshape.59
  247.0 3.3 all-to-all-start.1
  250.6 9.3 %reduce = f32[2048,4]{1,0:T(8,128)S(1)} reduce(f32[2048,1,4]{2,1,0:T(1,128)S(1)} %bitcast.55, f32[]{:T(128)} %broadcast.98), dimensions={1}, to_apply=%bitcast.43.reduce_sub_computation | reduce | bytes 65540
  260.0 1.4 reshape.61
  261.3 3.3 all-to-all-start.2
  264.6 4.6 maximum_bitcast_fusion
  269.2 5.2 copy.37
  274.5 4.9 all-to-all-start
  279.8 0.7 reduce.3
  280.5 1.7 reshape.60
  282.7 0.7 reduce.1
  283.5 1.7 reshape.62
  285.5 42.0 %all-to-all-done = f32[1,2048,4,128]{3,2,0,1:T(4,128)} async-done(((f32[1,2048,4,128]{3,2,0,1:T(4,128)}), f32[1,2048,4,128]{3,2,0,1:T(4,128)}, u32[]{:S(2)}, u32[]{:S(2)}) %all-to-all-start) | async-done | bytes 4194336 | tf_op jit(solution)/shard_map/all_to_all | solution.py:68
  327.5 5.3 copy.41
  332.9 5.1 multiply_reduce_fusion.1
  338.1 4.5 convolution_convert_fusion.1
  343.3 0.5 all-gather.11.cloned.1.call-update
  344.1 155.1 %all-reduce.2.cloned.1.call-done = bf16[512,4096]{1,0:T(8,128)(2,1)} async-done(((bf16[512,4096]{1,0:T(8,128)(2,1)}), bf16[512,4096]{1,0:T(8,128)(2,1)}) %all-reduce.2.cloned.1.call-update) | async-done | bytes 4194320 | tf_op jit(solution)/shard_map/psum | solution.py:80
  499.2 9.2 %convert_add_fusion = (f32[512,4096]{1,0:T(8,128)}, f32[512]{0:T(512)S(1)}) fusion(bf16[512,4096]{1,0:T(8,128)(2,1)} %all-gather.5.cloned.1.call-done, bf16[512,4096]{1,0:T(8,128)(2,1)} %all-reduce.2.cloned.1.call-done), kind=kLoop, calls=%fused_computation.14 | loop fusion | flops 10485248 | bytes 16779264 | tf_op jit(solution)/shard_map/add | solution.py:83
  508.4 131.6 %all-gather.9.cloned.1.call-done = bf16[4096,2,1376]{0,2,1:T(8,128)(2,1)} async-done(((bf16[1024,2,1376]{0,2,1:T(8,128)(2,1)}), bf16[4096,2,1376]{0,2,1:T(8,128)(2,1)}) %all-gather.9.cloned.1.call-update) | async-done | bytes 22544400 | tf_op jit(solution)/shard_map/all_gather | solution.py:89
  639.9 20.5 %fusion.16 = f32[512,2,1376]{0,2,1:T(8,128)} fusion(bf16[4096,2,1376]{0,2,1:T(8,128)(2,1)} %all-gather.9.cloned.1.call-done, f32[4096]{0:T(1024)S(1)} %copy-done.6, f32[512]{0:T(512)S(1)} %add_rsqrt_fusion, bf16[512,4096]{1,0:T(8,128)(2,1)} %all-gather.5.cloned.1.call-done, bf16[512,4096]{1,0:T(8,128)(2,1)} %all-reduce.2.cloned.1.call-done), kind=kOutput, calls=%fused_computation.25 | convolution fusion | flops 11555307520 | bytes 36587520 | tf_op jit(solution)/shard_map/td,dgf->tgf/dot_general | solution.py:86
  660.4 55.6 %all-gather.11.cloned.1.call-done = bf16[1376,4096]{1,0:T(8,128)(2,1)} async-done(((bf16[1376,1024]{1,0:T(8,128)(2,1)}), bf16[1376,4096]{1,0:T(8,128)(2,1)}) %all-gather.11.cloned.1.call-update) | async-done | bytes 11272208 | tf_op jit(solution)/shard_map/all_gather | solution.py:95
  716.0 13.6 %convolution_convert_fusion = bf16[512,4096]{1,0:T(8,128)(2,1)} fusion(bf16[1376,4096]{1,0:T(8,128)(2,1)} %all-gather.11.cloned.1.call-done, f32[512,2,1376]{0,2,1:T(8,128)} %fusion.16), kind=kOutput, calls=%fused_computation.22 | convolution fusion | flops 5777686528 | bytes 21102592 | tf_op jit(solution)/shard_map/dot_general | solution.py:93
  729.6 88.4 %reduce-scatter.2.cloned.1.call-done = bf16[64,4096]{1,0:T(8,128)(2,1)} async-done(((bf16[512,4096]{1,0:T(8,128)(2,1)}), bf16[64,4096]{1,0:T(8,128)(2,1)}) %reduce-scatter.2.cloned.1.call-update) | async-done | bytes 524304 | tf_op jit(solution)/shard_map/reduce_scatter | solution.py:98
  818.0 2.3 add_convert_fusion
  (43 shorter events, 3.7 us)
Async XLA Ops:
  6.5 78.5 %all-gather.5.cloned.1.call-start = ((), (), s32[]{:S(2)}) async-start(), calls=%async_computation.4 | async-start | bytes 4718592 | tf_op jit(solution)/shard_map/all_gather | solution.py:23
  7.3 114.9 %all-gather.7.cloned.1.call-start = ((), (), s32[]{:S(2)}) async-start(), calls=%async_computation.5 | async-start | bytes 2621440 | tf_op jit(solution)/shard_map/all_gather | solution.py:31
  7.3 80.8 %copy-start.5 = (f32[4096]{0:T(1024)S(1)}, f32[4096]{0:T(1024)}, u32[]{:S(2)}) copy-start(f32[4096]{0:T(1024)} %param.10) | copy-start | bytes 49156
  107.4 7.1 copy-start.4
  141.8 19.2 %copy-start.2 = (bf16[1,2048,4,128]{1,3,2,0:T(8,128)(2,1)S(1)}, bf16[1,2048,4,128]{1,3,2,0:T(8,128)(2,1)}, u32[]{:S(2)}) copy-start(bf16[1,2048,4,128]{1,3,2,0:T(8,128)(2,1)} %copy.49) | copy-start | bytes 6291460
  141.8 19.2 %copy-start.3 = (bf16[512,4,128]{0,2,1:T(8,128)(2,1)S(1)}, bf16[512,4,128]{0,2,1:T(8,128)(2,1)}, u32[]{:S(2)}) copy-start(bf16[512,4,128]{0,2,1:T(8,128)(2,1)} %copy.45) | copy-start | bytes 1572868
  198.0 19.2 %copy-start.1 = (bf16[1,2048,4,128]{1,3,2,0:T(8,128)(2,1)S(1)}, bf16[1,2048,4,128]{1,3,2,0:T(8,128)(2,1)}, u32[]{:S(2)}) copy-start(bf16[1,2048,4,128]{1,3,2,0:T(8,128)(2,1)} %copy.44) | copy-start | bytes 6291460
  247.0 14.4 %all-to-all-start.1 = ((f32[4,1,2048]{2,1,0:T(1,128)}), f32[4,1,2048]{2,1,0:T(1,128)S(1)}, u32[]{:S(2)}, u32[]{:S(2)}) async-start(f32[4,1,2048]{2,1,0:T(1,128)} %reshape.59), calls=%async_computation.1 | async-start | bytes 65536 | tf_op jit(solution)/shard_map/all_to_all | solution.py:66
  261.3 13.2 %all-to-all-start.2 = ((f32[4,1,2048]{2,1,0:T(1,128)}), f32[4,1,2048]{2,1,0:T(1,128)S(1)}, u32[]{:S(2)}, u32[]{:S(2)}) async-start(f32[4,1,2048]{2,1,0:T(1,128)} %reshape.61), calls=%async_computation.2 | async-start | bytes 65536 | tf_op jit(solution)/shard_map/all_to_all | solution.py:67
  274.5 53.1 %all-to-all-start = ((f32[1,2048,4,128]{3,2,0,1:T(4,128)}), f32[1,2048,4,128]{3,2,0,1:T(4,128)}, u32[]{:S(2)}, u32[]{:S(2)}) async-start(f32[1,2048,4,128]{3,2,0,1:T(4,128)} %copy.37), calls=%async_computation | async-start | bytes 8388608 | tf_op jit(solution)/shard_map/all_to_all | solution.py:68
  279.3 219.8 %all-reduce.2.cloned.1.call-start = ((), (), s32[]{:S(2)}) async-start(), calls=%async_computation.6 | async-start | bytes 8388608 | tf_op jit(solution)/shard_map/psum | solution.py:80
  332.9 5.3 copy-start
  342.7 297.3 %all-gather.9.cloned.1.call-start = ((), (), s32[]{:S(2)}) async-start(), calls=%async_computation.7 | async-start | bytes 28180480 | tf_op jit(solution)/shard_map/all_gather | solution.py:89
  343.2 372.8 %all-gather.11.cloned.1.call-start = ((), (), s32[]{:S(2)}) async-start(), calls=%async_computation.8 | async-start | bytes 14090240 | tf_op jit(solution)/shard_map/all_gather | solution.py:95
  343.8 296.1 %copy-start.6 = (f32[4096]{0:T(1024)S(1)}, f32[4096]{0:T(1024)}, u32[]{:S(2)}) copy-start(f32[4096]{0:T(1024)} %param.15) | copy-start | bytes 49156
  343.8 474.2 %reduce-scatter.2.cloned.1.call-start = ((), (), s32[]{:S(2)}) async-start(), calls=%async_computation.9 | async-start | bytes 4718592 | tf_op jit(solution)/shard_map/reduce_scatter | solution.py:98
Sparse Core Ops, SparseCore 0:
  9.5 75.5 all-gather.4
  101.0 21.0 all-gather.6
  342.8 156.3 all-reduce.1
  500.6 139.2 all-gather.8
  641.3 74.6 all-gather.10
  729.7 88.2 reduce-scatter.1
where the time goes:
time: 835 us; the launch traced here: 827 us
  waiting for transfers between devices  540 us (65%)
  matrix products  124 us (15%)
  other arithmetic  84.6 us (10%)
  local copies, waits for them, and re-layouts  52.2 us (6%)
  between operations  13.9 us (2%)
  starting transfers between devices  12.2 us (1%)
    psum x1, waiting for transfers between devices, per_device(): lax.psum(jnp.dot(attended, w_out, preferred_element_type=jnp.float32).ast...  155 us
    all_gather x1, waiting for transfers between devices, per_device(): lax.all_gather(w_gate_up, 'kv', axis=0, tiled=True)  132 us
    reduce_scatter x1, waiting for transfers between devices, per_device(): lax.psum_scatter(down_terms.astype(jnp.bfloat16), 'tp', scatter_dimension...  88.4 us
    all_gather x1, waiting for transfers between devices, per_device(): block_input = lax.all_gather(hidden_in, 'tp', axis=0, tiled=True)  65.3 us
    all_gather x1, waiting for transfers between devices, per_device(): lax.all_gather(w_down, 'kv', axis=1, tiled=True)  55.6 us
    all_to_all x1, waiting for transfers between devices, per_device(): lax.all_to_all(accum_all[None], 'kv', split_axis=1, concat_axis=0, tiled=...  42 us
    dot_general x2, matrix products, per_device(): jnp.einsum('qhd,khd->hqk', query_block, joined_key_rows, preferred_elemen...  38.7 us
    reduce_sum x2, other arithmetic, per_device(): masses.append(jnp.sum(raw_weights, axis=2).T)  38.4 us
  transfers between devices with their start and end apart: 9, of which 7 were waited for; matrix products, arithmetic and copies ran while one was open for 11% of the time, Pallas kernels for 0%

commit v1 on v0

--- a/solution.py
+++ b/solution.py
@@ -83,12 +83,21 @@
     residual = block_input.astype(jnp.float32) + heads_sum
     mlp_in = rms_scale(residual, gain_mlp)
     residual_own = lax.dynamic_slice_in_dim(residual, tp_index * own_rows, own_rows, 0)
-    gate_up = jnp.einsum(
-        "td,dgf->tgf",
-        mlp_in,
-        lax.all_gather(w_gate_up, "kv", axis=0, tiled=True),
-        preferred_element_type=jnp.float32,
-    )
+    peers, here, rows = (lax.axis_size("kv"), lax.axis_index("kv"), w_gate_up.shape[0])
+    ahead = [(i, (i + 1) % peers) for i in range(peers)]
+    carried, gate_up = (w_gate_up, None)
+    for step in range(peers):
+        coming = lax.ppermute(carried, "kv", ahead) if step < peers - 1 else None
+        update = jnp.einsum(
+            "td,dgf->tgf",
+            lax.dynamic_slice_in_dim(
+                mlp_in, (here - step) % peers * rows, carried.shape[0], axis=1
+            ),
+            carried,
+            preferred_element_type=jnp.float32,
+        )
+        gate_up = update if gate_up is None else gate_up + update
+        carried = coming
     activated = (jax.nn.silu(gate_up[:, 0, :]) * gate_up[:, 1, :]).astype(jnp.bfloat16)
     down_terms = jnp.dot(
         activated,

time: 835 us -> 715 us (0.86)
  waiting for transfers between devices: 540 us -> 411 us
    ppermute x0 -> x3, waiting for transfers between devices: none -> 174 us  [per_device(): coming = lax.ppermute(carried, 'kv', ahead) if step < peers - 1 else None]
    all_gather x1 -> x0, waiting for transfers between devices: 132 us -> none  [per_device(): lax.all_gather(w_gate_up, 'kv', axis=0, tiled=True)]
    psum x1, waiting for transfers between devices: 155 us -> 29.1 us  [per_device(): lax.psum(jnp.dot(attended, w_out, preferred_element_type=jnp.float32).ast...]
    all_gather x1, waiting for transfers between devices: 55.6 us -> 9.54 us  [per_device(): lax.all_gather(w_down, 'kv', axis=1, tiled=True)]
    dot_general x1 -> x4, matrix products: 20.5 us -> 28.5 us  [per_device(): jnp.einsum('td,dgf->tgf', lax.dynamic_slice_in_dim(mlp_in, (here - step)...]
    unnamed x25 -> x29, local copies, waits for them, and re-layouts: 28.1 us -> 28.1 us
  transfers between devices with their start and end apart: 9 -> 11, of which waited for: 7 -> 9; matrix products, arithmetic and copies ran while one was open for 11% -> 14% of each run, Pallas kernels for 0% -> 0%
where the time goes in v1:
time: 715 us; the launch traced here: 707 us
  waiting for transfers between devices  411 us (57%)
  matrix products  132 us (18%)
  other arithmetic  86.9 us (12%)
  local copies, waits for them, and re-layouts  52.3 us (7%)
  between operations  13.7 us (2%)
  starting transfers between devices  11.8 us (2%)
    ppermute x3, waiting for transfers between devices, per_device(): coming = lax.ppermute(carried, 'kv', ahead) if step < peers - 1 else None  174 us
    reduce_scatter x1, waiting for transfers between devices, per_device(): lax.psum_scatter(down_terms.astype(jnp.bfloat16), 'tp', scatter_dimension...  88.9 us
    all_gather x1, waiting for transfers between devices, per_device(): block_input = lax.all_gather(hidden_in, 'tp', axis=0, tiled=True)  65.3 us
    all_to_all x1, waiting for transfers between devices, per_device(): lax.all_to_all(accum_all[None], 'kv', split_axis=1, concat_axis=0, tiled=...  42.3 us
    reduce_sum x2, other arithmetic, per_device(): masses.append(jnp.sum(raw_weights, axis=2).T)  38.4 us
    dot_general x2, matrix products, per_device(): jnp.einsum('qhd,khd->hqk', query_block, joined_key_rows, preferred_elemen...  38.4 us
    dot_general x2, matrix products, per_device(): jnp.einsum('hqk,khd->qhd', raw_weights.astype(jnp.bfloat16), joined_value...  35.8 us
    psum x1, waiting for transfers between devices, per_device(): lax.psum(jnp.dot(attended, w_out, preferred_element_type=jnp.float32).ast...  29.1 us
  transfers between devices with their start and end apart: 11, of which 9 were waited for; matrix products, arithmetic and copies ran while one was open for 14% of the time, Pallas kernels for 0%

profile of v1, /device:TPU:0, one launch (start us, length us, event | category | flops | bytes accessed | tf_op | source)
XLA Modules:
  0.0 707.5 jit_solution(9438542337583224121)
XLA Ops:
  6.5 0.7 all-gather.4.cloned.1.call-update
  7.3 12.4 %copy.51 = bf16[512,8,4,384]{3,1,2,0:T(8,128)(2,1)} copy(bf16[512,8,4,384]{3,2,1,0:T(4,128)(2,1)} %bitcast.62) | data formatting | bytes 25165824
  19.7 65.3 %all-gather.4.cloned.1.call-done = bf16[512,4096]{1,0:T(8,128)(2,1)} async-done(((bf16[64,4096]{1,0:T(8,128)(2,1)}), bf16[512,4096]{1,0:T(8,128)(2,1)}) %all-gather.4.cloned.1.call-update) | async-done | bytes 4194320 | tf_op jit(solution)/shard_map/all_gather | solution.py:23
  85.0 3.1 fusion.12
  88.1 11.0 %fusion.19 = bf16[512,1536]{1,0:T(8,128)(2,1)S(1)} fusion(bf16[4096,1536]{1,0:T(8,128)(2,1)} %bitcast.63, bf16[512,4096]{1,0:T(8,128)(2,1)} %all-gather.4.cloned.1.call-done, f32[4096]{0:T(1024)S(1)} %copy-done.8, f32[512]{0:T(512)S(1)} %add_rsqrt_fusion.1), kind=kOutput, calls=%fused_computation.34 | convolution fusion | flops 6451625984 | bytes 18368512 | tf_op jit(solution)/shard_map/dot_general | solution.py:27
  100.0 0.9 copy.46
  100.9 6.4 fusion.71
  107.4 4.4 copy.44
  111.8 2.6 copy.49
  115.1 1.2 fusion.51
  116.4 4.2 copy_bitcast_fusion
  120.5 1.1 copy.45
  122.2 19.3 %fusion.1 = (f32[4,1024]{1,0:T(4,128)S(1)}, f32[4,1024,2560]{2,1,0:T(8,128)}) fusion(pred[2560]{0:T(1024)(128)(4,1)S(1)} %pad_add_fusion.1, bf16[512,4,128]{2,0,1:T(8,128)(2,1)S(1)} %copy.48, bf16[2048,4,128]{2,0,1:T(8,128)(2,1)} %get-tuple-element.26, bf16[2048,4,128]{2,0,1:T(8,128)(2,1)} %all-gather.6.cloned.1.call-done), kind=kOutput, calls=%fused_computation.5 | convolution fusion | flops 2721050624 | bytes 45632000 | tf_op jit(solution)/shard_map/qhd,khd->hqk/dot_general | solution.py:44
  141.5 19.2 %fusion.4 = f32[4,1024]{1,0:T(4,128)S(1)} fusion(f32[4,1024,2560]{2,1,0:T(8,128)} %get-tuple-element.19, f32[4,1024]{1,0:T(4,128)S(1)} %get-tuple-element.18, pred[2560]{0:T(1024)(128)(4,1)S(1)} %pad_add_fusion.1), kind=kLoop, calls=%fused_computation.8 | loop fusion | flops 52424704 | bytes 41978368 | tf_op jit(solution)/shard_map/reduce_sum | solution.py:53
  160.7 17.9 %fusion.33 = f32[1024,4,128]{0,2,1:T(8,128)} fusion(f32[4,1024,2560]{2,1,0:T(8,128)} %get-tuple-element.19, f32[4,1024]{1,0:T(4,128)S(1)} %get-tuple-element.18, pred[2560]{0:T(1024)(128)(4,1)S(1)} %pad_add_fusion.1, bf16[512,4,128]{0,2,1:T(8,128)(2,1)S(1)} %copy-done.5, bf16[2048,4,128]{0,2,1:T(8,128)(2,1)S(1)} %bitcast.71), kind=kOutput, calls=%fused_computation.48 | convolution fusion | flops 2742026240 | bytes 46680576 | tf_op jit(solution)/shard_map/hqk,khd->qhd/dot_general | solution.py:55
  178.6 19.1 %fusion = (f32[4,1024]{1,0:T(4,128)S(1)}, f32[4,1024,2560]{2,1,0:T(8,128)}) fusion(pred[2560]{0:T(1024)(128)(4,1)S(1)} %pad_add_fusion, bf16[512,4,128]{2,0,1:T(8,128)(2,1)S(1)} %copy.48, bf16[2048,4,128]{2,0,1:T(8,128)(2,1)S(1)} %get-tuple-element.27, bf16[2048,4,128]{2,0,1:T(8,128)(2,1)} %all-gather.6.cloned.1.call-done), kind=kOutput, calls=%fused_computation.4 | convolution fusion | flops 2721050624 | bytes 45632000 | tf_op jit(solution)/shard_map/qhd,khd->hqk/dot_general | solution.py:44
  197.7 19.2 %fusion.2 = f32[4,1024]{1,0:T(4,128)S(1)} fusion(f32[4,1024,2560]{2,1,0:T(8,128)} %get-tuple-element.21, f32[4,1024]{1,0:T(4,128)S(1)} %get-tuple-element.20, pred[2560]{0:T(1024)(128)(4,1)S(1)} %pad_add_fusion), kind=kLoop, calls=%fused_computation.6 | loop fusion | flops 52424704 | bytes 41978368 | tf_op jit(solution)/shard_map/reduce_sum | solution.py:53
  216.9 17.9 %fusion.30 = f32[1024,4,128]{0,2,1:T(8,128)} fusion(f32[4,1024,2560]{2,1,0:T(8,128)} %get-tuple-element.21, f32[4,1024]{1,0:T(4,128)S(1)} %get-tuple-element.20, pred[2560]{0:T(1024)(128)(4,1)S(1)} %pad_add_fusion, bf16[512,4,128]{0,2,1:T(8,128)(2,1)S(1)} %copy-done.5, bf16[2048,4,128]{0,2,1:T(8,128)(2,1)S(1)} %bitcast.70), kind=kOutput, calls=%fused_computation.47 | convolution fusion | flops 2742026240 | bytes 46680576 | tf_op jit(solution)/shard_map/hqk,khd->qhd/dot_general | solution.py:55
  235.7 9.7 %reduce.2 = f32[2048,4]{1,0:T(8,128)S(1)} reduce(f32[2048,1,4]{2,1,0:T(1,128)S(1)} %bitcast.66, f32[]{:T(128)} %broadcast.102), dimensions={1}, to_apply=%bitcast.50.reduce_sub_computation | reduce | bytes 65540
  245.5 1.3 reshape.62
  246.8 3.3 all-to-all-start.1
  250.5 9.3 %reduce = f32[2048,4]{1,0:T(8,128)S(1)} reduce(f32[2048,1,4]{2,1,0:T(1,128)S(1)} %bitcast.67, f32[]{:T(128)} %broadcast.102), dimensions={1}, to_apply=%bitcast.52.reduce_sub_computation | reduce | bytes 65540
  259.8 1.4 reshape.64
  261.2 3.3 all-to-all-start.2
  264.4 4.6 maximum_bitcast_fusion
  269.1 5.2 copy.37
  274.3 4.9 all-to-all-start
  280.1 1.7 reshape.63
  282.3 0.7 reduce.1
  283.0 1.7 reshape.65
  285.1 42.3 %all-to-all-done = f32[1,2048,4,128]{3,2,0,1:T(4,128)} async-done(((f32[1,2048,4,128]{3,2,0,1:T(4,128)}), f32[1,2048,4,128]{3,2,0,1:T(4,128)}, u32[]{:S(2)}, u32[]{:S(2)}) %all-to-all-start) | async-done | bytes 4194336 | tf_op jit(solution)/shard_map/all_to_all | solution.py:68
  327.4 5.3 copy.41
  332.7 5.1 multiply_reduce_fusion.1
  338.0 4.5 convolution_convert_fusion.1
  343.1 63.2 %collective-permute-done = bf16[1024,2,1376]{0,2,1:T(8,128)(2,1)} collective-permute-done((bf16[1024,2,1376]{0,2,1:T(8,128)(2,1)}, bf16[1024,2,1376]{0,2,1:T(8,128)(2,1)}, u32[]{:S(2)}, u32[]{:S(2)}) %collective-permute-start) | collective-permute-done | bytes 5636128 | tf_op jit(solution)/shard_map/ppermute | solution.py:90
  406.3 63.7 %collective-permute-done.1 = bf16[1024,2,1376]{0,2,1:T(8,128)(2,1)} collective-permute-done((bf16[1024,2,1376]{0,2,1:T(8,128)(2,1)}, bf16[1024,2,1376]{0,2,1:T(8,128)(2,1)}, u32[]{:S(2)}, u32[]{:S(2)}) %collective-permute-start.1) | collective-permute-done | bytes 5636128 | tf_op jit(solution)/shard_map/ppermute | solution.py:90
  470.0 29.1 %all-reduce.2.cloned.1.call-done = bf16[512,4096]{1,0:T(8,128)(2,1)} async-done(((bf16[512,4096]{1,0:T(8,128)(2,1)}), bf16[512,4096]{1,0:T(8,128)(2,1)}) %all-reduce.2.cloned.1.call-update) | async-done | bytes 4194320 | tf_op jit(solution)/shard_map/psum | solution.py:80
  499.0 8.9 %convert_add_fusion = (f32[512,4096]{1,0:T(8,128)}, f32[512]{0:T(512)S(1)}) fusion(bf16[512,4096]{1,0:T(8,128)(2,1)} %all-gather.4.cloned.1.call-done, bf16[512,4096]{1,0:T(8,128)(2,1)} %all-reduce.2.cloned.1.call-done), kind=kLoop, calls=%fused_computation.14 | loop fusion | flops 10485248 | bytes 16779264 | tf_op jit(solution)/shard_map/add | solution.py:83
  508.0 2.4 multiply_convert_fusion
  510.4 6.3 fusion.45
  516.7 5.3 fusion.41
  522.0 7.7 %fusion.43 = f32[512,2,1376]{0,2,1:T(8,128)} fusion(bf16[1024,2,1376]{0,2,1:T(8,128)(2,1)} %collective-permute-done, bf16[512,4096]{1,0:T(8,128)(2,1)S(1)} %multiply_convert_fusion, s32[]{:T(128)S(6)} %select_n.61), kind=kOutput, calls=%fused_computation.55 | convolution fusion | flops 2885681152 | bytes 12320772 | tf_op jit(solution)/shard_map/td,dgf->tgf/dot_general | solution.py:91
  529.7 47.4 %collective-permute-done.2 = bf16[1024,2,1376]{0,2,1:T(8,128)(2,1)} collective-permute-done((bf16[1024,2,1376]{0,2,1:T(8,128)(2,1)}, bf16[1024,2,1376]{0,2,1:T(8,128)(2,1)}, u32[]{:S(2)}, u32[]{:S(2)}) %collective-permute-start.2) | collective-permute-done | bytes 5636128 | tf_op jit(solution)/shard_map/ppermute | solution.py:90
  577.1 9.3 %add_add_fusion = f32[512,2,1376]{0,2,1:T(8,128)} fusion(f32[512,2,1376]{0,2,1:T(8,128)S(1)} %fusion.41, f32[512,2,1376]{0,2,1:T(8,128)S(1)} %fusion.45, f32[512,2,1376]{0,2,1:T(8,128)} %fusion.43, bf16[1024,2,1376]{0,2,1:T(8,128)(2,1)} %collective-permute-done.2, bf16[512,4096]{1,0:T(8,128)(2,1)S(1)} %multiply_convert_fusion, s32[]{:T(128)S(6)} %select_n.65), kind=kOutput, calls=%fused_computation.24 | convolution fusion | flops 2889908224 | bytes 29229060 | tf_op jit(solution)/shard_map/td,dgf->tgf/dot_general | solution.py:91
  586.3 9.5 %all-gather.8.cloned.1.call-done = bf16[1376,4096]{1,0:T(8,128)(2,1)} async-done(((bf16[1376,1024]{1,0:T(8,128)(2,1)}), bf16[1376,4096]{1,0:T(8,128)(2,1)}) %all-gather.8.cloned.1.call-update) | async-done | bytes 11272208 | tf_op jit(solution)/shard_map/all_gather | solution.py:104
  595.9 13.7 %convolution_convert_fusion = bf16[512,4096]{1,0:T(8,128)(2,1)} fusion(bf16[1376,4096]{1,0:T(8,128)(2,1)} %all-gather.8.cloned.1.call-done, f32[512,2,1376]{0,2,1:T(8,128)} %add_add_fusion), kind=kOutput, calls=%fused_computation.22 | convolution fusion | flops 5777686528 | bytes 21102592 | tf_op jit(solution)/shard_map/dot_general | solution.py:102
  609.6 88.9 %reduce-scatter.2.cloned.1.call-done = bf16[64,4096]{1,0:T(8,128)(2,1)} async-done(((bf16[512,4096]{1,0:T(8,128)(2,1)}), bf16[64,4096]{1,0:T(8,128)(2,1)}) %reduce-scatter.2.cloned.1.call-update) | async-done | bytes 524304 | tf_op jit(solution)/shard_map/reduce_scatter | solution.py:107
  698.5 2.3 add_convert_fusion
  (54 shorter events, 6.1 us)
Async XLA Ops:
  6.5 78.5 %all-gather.4.cloned.1.call-start = ((), (), s32[]{:S(2)}) async-start(), calls=%async_computation.4 | async-start | bytes 4718592 | tf_op jit(solution)/shard_map/all_gather | solution.py:23
  7.3 114.9 %all-gather.6.cloned.1.call-start = ((), (), s32[]{:S(2)}) async-start(), calls=%async_computation.5 | async-start | bytes 2621440 | tf_op jit(solution)/shard_map/all_gather | solution.py:31
  7.3 80.8 %copy-start.8 = (f32[4096]{0:T(1024)S(1)}, f32[4096]{0:T(1024)}, u32[]{:S(2)}) copy-start(f32[4096]{0:T(1024)} %param.10) | copy-start | bytes 49156
  107.4 7.1 %copy-start.7 = (s32[2]{0:T(128)S(1)}, s32[2]{0:T(128)}, u32[]{:S(2)}) copy-start(s32[2]{0:T(128)} %param.13) | copy-start | bytes 28
  141.5 19.2 %copy-start.4 = (bf16[1,2048,4,128]{1,3,2,0:T(8,128)(2,1)S(1)}, bf16[1,2048,4,128]{1,3,2,0:T(8,128)(2,1)}, u32[]{:S(2)}) copy-start(bf16[1,2048,4,128]{1,3,2,0:T(8,128)(2,1)} %copy.49) | copy-start | bytes 6291460
  141.5 19.2 %copy-start.5 = (bf16[512,4,128]{0,2,1:T(8,128)(2,1)S(1)}, bf16[512,4,128]{0,2,1:T(8,128)(2,1)}, u32[]{:S(2)}) copy-start(bf16[512,4,128]{0,2,1:T(8,128)(2,1)} %copy.45) | copy-start | bytes 1572868
  197.7 19.2 %copy-start.3 = (bf16[1,2048,4,128]{1,3,2,0:T(8,128)(2,1)S(1)}, bf16[1,2048,4,128]{1,3,2,0:T(8,128)(2,1)}, u32[]{:S(2)}) copy-start(bf16[1,2048,4,128]{1,3,2,0:T(8,128)(2,1)} %copy.44) | copy-start | bytes 6291460
  246.8 14.3 %all-to-all-start.1 = ((f32[4,1,2048]{2,1,0:T(1,128)}), f32[4,1,2048]{2,1,0:T(1,128)S(1)}, u32[]{:S(2)}, u32[]{:S(2)}) async-start(f32[4,1,2048]{2,1,0:T(1,128)} %reshape.62), calls=%async_computation.1 | async-start | bytes 65536 | tf_op jit(solution)/shard_map/all_to_all | solution.py:66
  261.2 13.2 %all-to-all-start.2 = ((f32[4,1,2048]{2,1,0:T(1,128)}), f32[4,1,2048]{2,1,0:T(1,128)S(1)}, u32[]{:S(2)}, u32[]{:S(2)}) async-start(f32[4,1,2048]{2,1,0:T(1,128)} %reshape.64), calls=%async_computation.2 | async-start | bytes 65536 | tf_op jit(solution)/shard_map/all_to_all | solution.py:67
  274.3 53.1 %all-to-all-start = ((f32[1,2048,4,128]{3,2,0,1:T(4,128)}), f32[1,2048,4,128]{3,2,0,1:T(4,128)}, u32[]{:S(2)}, u32[]{:S(2)}) async-start(f32[1,2048,4,128]{3,2,0,1:T(4,128)} %copy.37), calls=%async_computation | async-start | bytes 8388608 | tf_op jit(solution)/shard_map/all_to_all | solution.py:68
  279.2 219.9 %all-reduce.2.cloned.1.call-start = ((), (), s32[]{:S(2)}) async-start(), calls=%async_computation.6 | async-start | bytes 8388608 | tf_op jit(solution)/shard_map/psum | solution.py:80
  332.7 5.3 copy-start.2
  342.5 253.4 %all-gather.8.cloned.1.call-start = ((), (), s32[]{:S(2)}) async-start(), calls=%async_computation.7 | async-start | bytes 14090240 | tf_op jit(solution)/shard_map/all_gather | solution.py:104
  342.5 63.7 %collective-permute-start = (bf16[1024,2,1376]{0,2,1:T(8,128)(2,1)}, bf16[1024,2,1376]{0,2,1:T(8,128)(2,1)}, u32[]{:S(2)}, u32[]{:S(2)}) collective-permute-start(bf16[1024,2,1376]{0,2,1:T(8,128)(2,1)} %param.16), channel_id=1, source_target_pairs={{0,1},{1,2},{2,3},{3,0},{4,5},{5,6},{6,7},{7,4},{8,9},{9,10},{10,1... | collective-permute-start | bytes 16908296 | tf_op jit(solution)/shard_map/ppermute | solution.py:90
  343.1 355.4 %reduce-scatter.2.cloned.1.call-start = ((), (), s32[]{:S(2)}) async-start(), calls=%async_computation.8 | async-start | bytes 4718592 | tf_op jit(solution)/shard_map/reduce_scatter | solution.py:107
  406.3 63.7 %collective-permute-start.1 = (bf16[1024,2,1376]{0,2,1:T(8,128)(2,1)}, bf16[1024,2,1376]{0,2,1:T(8,128)(2,1)}, u32[]{:S(2)}, u32[]{:S(2)}) collective-permute-start(bf16[1024,2,1376]{0,2,1:T(8,128)(2,1)} %collective-permute-done), channel_id=1, source_target_pairs={{0,1},{1,2},{2,3},{3,0},{4,5},{5,6},{6,7},{7,4},{8,9},{9,10},{10,1... | collective-permute-start | bytes 16908296 | tf_op jit(solution)/shard_map/ppermute | solution.py:90
  470.0 107.1 %collective-permute-start.2 = (bf16[1024,2,1376]{0,2,1:T(8,128)(2,1)}, bf16[1024,2,1376]{0,2,1:T(8,128)(2,1)}, u32[]{:S(2)}, u32[]{:S(2)}) collective-permute-start(bf16[1024,2,1376]{0,2,1:T(8,128)(2,1)} %collective-permute-done.1), channel_id=1, source_target_pairs={{0,1},{1,2},{2,3},{3,0},{4,5},{5,6},{6,7},{7,4},{8,9},{9,10},{10,1... | collective-permute-start | bytes 16908296 | tf_op jit(solution)/shard_map/ppermute | solution.py:90
  470.0 38.0 %copy-start.6 = (f32[4096]{0:T(1024)S(1)}, f32[4096]{0:T(1024)}, u32[]{:S(2)}) copy-start(f32[4096]{0:T(1024)} %param.15) | copy-start | bytes 49156
  499.0 9.0 %copy-start = (bf16[512,4096]{1,0:T(8,128)(2,1)S(1)}, bf16[512,4096]{1,0:T(8,128)(2,1)}, u32[]{:S(2)}) copy-start(bf16[512,4096]{1,0:T(8,128)(2,1)} %all-gather.4.cloned.1.call-done) | copy-start | bytes 12582916
  499.0 9.0 %copy-start.1 = (bf16[512,4096]{1,0:T(8,128)(2,1)S(1)}, bf16[512,4096]{1,0:T(8,128)(2,1)}, u32[]{:S(2)}) copy-start(bf16[512,4096]{1,0:T(8,128)(2,1)} %all-reduce.2.cloned.1.call-done) | copy-start | bytes 12582916
Sparse Core Ops, SparseCore 0:
  9.5 75.5 all-gather.3
  101.0 21.0 all-gather.5
  342.6 156.3 all-reduce.1
  500.5 95.3 all-gather.7
  609.7 88.7 reduce-scatter.1
